TPU v7x, 32 devices: a whole 2x2x4 slice. The times are simulated.
32 devices in a mesh: dp: 4 (over z), ctx: 4 (over y, core), tp: 2 (over x).
Axes of the slice: x: 2, y: 2, z: 4, core: 2. Of those that a mesh axis runs over, the one named last changes fastest.
Arguments:
- queries: bfloat16 [4, 512, 4096], P('dp', 'ctx', 'tp'), may hold values from -8 to 8
- keys_text: bfloat16 [4, 512, 512], P('dp', 'ctx', 'tp'), may hold values from -8 to 8
- values_text: bfloat16 [4, 512, 512], P('dp', 'ctx', 'tp'), may hold values from -6 to 6
- patch_rows: bfloat16 [4, 4, 8, 2, 512], P('dp', 'ctx', None, None, 'tp'), may hold values from -6 to 6
- patch_owner: int32 [4, 4, 8, 1], P('dp', 'ctx'), may hold values from 0 to 3; in each aligned block of 8 rows (0 to 7, 8 to 15, ..., all dimensions but the last counted through in order) at most 4 rows name the same one
- patch_place: int32 [4, 4, 8], P('dp', 'ctx'), may hold values from 0 to 127
- value_head: bfloat16 [4096], P('tp'), may hold values from -0.75 to 0.75
Outputs:
- attention: bfloat16 [4, 512, 4096], P('dp', 'ctx', 'tp')
- value_out: float32 [4, 512], P('dp', 'ctx')
Inputs may be any that keep to these rules, and one draw needn't show every extreme that they name: `patch_owner`: among the rows of one vision shard at most 4 name the same sequence, and exactly 4 do in some shards. `patch_place`: rows that share an owner, a ctx index and a position are all added there.
All inputs are finite; a program needn't handle non-finite values.
Results may differ from a plain program's by a relative error of at most 0.0079.
Values may be sent and summed in bfloat16 or wider, within the bound.
A program may use at most 64 MiB of HBM per device.

v0:
```python
import jax
import jax.numpy as jnp
from jax import lax
from jax.sharding import PartitionSpec as P

HD = 128
CAP = 4


def attend_block(
    carried, query_split, query_place, block_keys, block_values, key_place, score_scale
):
    running_max, denominator, numerator = carried
    scores = (
        jnp.einsum("tgrd,sgd->tgrs", query_split, block_keys, preferred_element_type=jnp.float32)
        * score_scale
    )
    allowed = (key_place[None, :] <= query_place[:, None])[:, None, None, :]
    scores = jnp.where(allowed, scores, -1e30)
    new_max = jnp.maximum(running_max, jnp.max(scores, axis=-1))
    weights = jnp.where(allowed, jnp.exp(scores - new_max[..., None]), 0.0)
    shrink = jnp.exp(running_max - new_max)
    denominator = denominator * shrink + jnp.sum(weights, axis=-1)
    numerator = numerator * shrink[..., None] + jnp.einsum(
        "tgrs,sgd->tgrd",
        weights.astype(jnp.bfloat16),
        block_values,
        preferred_element_type=jnp.float32,
    )
    return (new_max, denominator, numerator)


def unchanged(carried):
    return carried


def body(queries, keys_text, values_text, patch_rows, patch_owner, patch_place, value_head):
    token_count = queries.shape[1]
    kv_width = keys_text.shape[2]
    groups = kv_width // HD
    head_count = queries.shape[2] // HD
    group_size = head_count // groups
    score_scale = HD ** (-0.5)
    dp_count = lax.axis_size("dp")
    slot_count = dp_count * CAP
    owner_seq = patch_owner[0, 0, :, 0]
    places = patch_place[0, 0]
    owner_hits = (owner_seq[:, None] == jnp.arange(dp_count, dtype=jnp.int32)[None, :]).astype(
        jnp.int32
    )
    before = jnp.cumsum(owner_hits, axis=0) - owner_hits
    slot_rank = jnp.sum(before * owner_hits, axis=1)
    target = owner_seq * CAP + slot_rank
    select = (jnp.arange(slot_count, dtype=jnp.int32)[:, None] == target[None, :]).astype(jnp.int32)
    row_data = patch_rows[0, 0].reshape(places.shape[0], 2 * kv_width)
    packed = jnp.dot(
        select.astype(jnp.bfloat16), row_data, preferred_element_type=jnp.float32
    ).astype(jnp.bfloat16)
    filled = jnp.sum(select, axis=1)
    slot_place = jnp.sum(select * places[None, :], axis=1) + (1 - filled) * token_count
    packed = packed.reshape(slot_count, 2, kv_width)
    arrived, arrived_place = (
        lax.all_to_all(packed, "dp", split_axis=0, concat_axis=0, tiled=True),
        lax.all_to_all(slot_place, "dp", split_axis=0, concat_axis=0, tiled=True),
    )
    landing = (jnp.arange(token_count, dtype=jnp.int32)[:, None] == arrived_place[None, :]).astype(
        jnp.bfloat16
    )
    arrivals = jnp.dot(
        landing, arrived.reshape(slot_count, 2 * kv_width), preferred_element_type=jnp.float32
    )
    merged_keys = (keys_text[0].astype(jnp.float32) + arrivals[:, :kv_width]).astype(jnp.bfloat16)
    merged_values = (values_text[0].astype(jnp.float32) + arrivals[:, kv_width:]).astype(
        jnp.bfloat16
    )
    query_split = queries[0].reshape(token_count, groups, group_size, HD)
    first_row = lax.axis_index("ctx") * token_count
    query_place = first_row + jnp.arange(token_count, dtype=jnp.int32)
    initial = (
        jnp.full((token_count, groups, group_size), -1e30, jnp.float32),
        jnp.zeros((token_count, groups, group_size), jnp.float32),
        jnp.zeros((token_count, groups, group_size, HD), jnp.float32),
    )
    carried = initial
    start_row = jnp.int32(0)
    piece_keys = lax.all_gather(merged_keys, "ctx", axis=0, tiled=True)
    piece_values = lax.all_gather(merged_values, "ctx", axis=0, tiled=True)
    piece_rows = piece_keys.shape[0]
    block_rows = min(512, piece_rows)
    for lower in range(0, piece_rows, block_rows):
        upper = min(lower + block_rows, piece_rows)
        block_keys = piece_keys[lower:upper].reshape(upper - lower, groups, HD)
        block_values = piece_values[lower:upper].reshape(upper - lower, groups, HD)
        key_place = start_row + lower + jnp.arange(upper - lower, dtype=jnp.int32)

        def update(state_in):
            return attend_block(
                state_in, query_split, query_place, block_keys, block_values, key_place, score_scale
            )

        carried = lax.cond(
            start_row + lower <= first_row + token_count - 1, update, unchanged, carried
        )
    running_max, denominator, numerator = carried
    attention = (
        (numerator / denominator[..., None])
        .reshape(token_count, head_count * HD)
        .astype(jnp.bfloat16)
    )
    partial_value = jnp.dot(attention, value_head, preferred_element_type=jnp.float32)
    value_out = lax.psum(partial_value, "tp")
    return (attention[None], value_out[None])


def solution(mesh):
    in_specs = (
        P("dp", "ctx", "tp"),
        P("dp", "ctx", "tp"),
        P("dp", "ctx", "tp"),
        P("dp", "ctx", None, None, "tp"),
        P("dp", "ctx", None, None),
        P("dp", "ctx", None),
        P("tp"),
    )
    out_specs = (P("dp", "ctx", "tp"), P("dp", "ctx"))
    return jax.shard_map(body, mesh=mesh, in_specs=in_specs, out_specs=out_specs, check_vma=False)
```

profile of v0, /device:TPU:0, one launch (start us, length us, event | category | flops | bytes accessed | tf_op | source)
XLA Modules:
  0.0 53.5 jit_solution(15466480431015100622)
XLA Ops:
  0.6 0.7 %fusion.25 = s32[8,4]{0,1:T(4,128)S(1)} fusion(s32[8]{0:T(128)} %bitcast.58), kind=kLoop, calls=%fused_computation.37 | loop fusion | flops 64 | bytes 160 | tf_op jit(solution)/shard_map/convert_element_type | solution.py:48
  1.3 0.2 reduce_window_sum.11
  1.5 0.7 %select_reduce_fusion.1 = s32[8]{0:T(128)S(1)} fusion(s32[8,4]{0,1:T(4,128)S(1)} %reduce_window_sum.11, s32[8]{0:T(128)} %bitcast.59), kind=kLoop, calls=%fused_computation.35 | loop fusion | flops 152 | bytes 192 | tf_op jit(solution)/shard_map/reduce_sum | solution.py:52
  2.2 0.7 %multiply_add_fusion.1 = s32[8]{0:T(128)S(1)} fusion(s32[8]{0:T(128)S(1)} %select_reduce_fusion.1, s32[1,1,8,1]{2,3,1,0:T(1,128)} %param.13), kind=kLoop, calls=%fused_computation.39 | loop fusion | flops 16 | bytes 96 | tf_op jit(solution)/shard_map/add | solution.py:53
  2.8 0.7 %convert_reduce_fusion = (s32[16]{0:T(128)S(1)}, s32[16]{0:T(128)S(1)}) fusion(s32[8]{0:T(128)S(1)} %multiply_add_fusion.1, s32[8]{0:T(128)} %bitcast.60), kind=kLoop, calls=%fused_computation.31 | loop fusion | flops 608 | bytes 192 | tf_op jit(solution)/shard_map/reduce_sum | solution.py:59
  3.6 0.7 %add.48 = s32[4,4,1]{1,0,2:T(4,128)} reshape(s32[16]{0:T(128)S(1)} %multiply_add_fusion) | data formatting | bytes 128 | tf_op jit(solution)/shard_map/add | solution.py:60
  4.2 6.3 %all-to-all-start = ((s32[4,4,1]{1,2,0:T(1,128)}), s32[4,4,1]{1,2,0:T(1,128)S(1)}, u32[]{:S(2)}, u32[]{:S(2)}) async-start(s32[4,4,1]{1,2,0:T(1,128)} %bitcast.7), calls=%async_computation | async-start | bytes 4096 | tf_op jit(solution)/shard_map/all_to_all | solution.py:64
  10.6 0.7 %copy.45 = bf16[1,8,2,256]{3,1,2,0:T(8,128)(2,1)S(1)} copy(bf16[1,8,2,256]{3,2,1,0:T(2,128)(2,1)} %bitcast.56) | data formatting | bytes 16384
  11.3 0.3 convolution_convert_fusion
  11.5 0.6 %reshape.108 = bf16[16,2,256]{2,1,0:T(2,128)(2,1)} reshape(bf16[16,512]{1,0:T(8,128)(2,1)S(1)} %convolution_convert_fusion) | data formatting | bytes 32768 | tf_op jit(solution)/shard_map/reshape | solution.py:61
  12.2 3.8 %all-to-all-done = s32[4,4,1]{1,2,0:T(1,128)S(1)} async-done(((s32[4,4,1]{1,2,0:T(1,128)}), s32[4,4,1]{1,2,0:T(1,128)S(1)}, u32[]{:S(2)}, u32[]{:S(2)}) %all-to-all-start) | async-done | bytes 96 | tf_op jit(solution)/shard_map/all_to_all | solution.py:64
  16.0 3.3 %all-to-all-start.1 = ((bf16[16,2,256]{2,1,0:T(2,128)(2,1)}), bf16[16,2,256]{2,1,0:T(2,128)(2,1)S(1)}, u32[]{:S(2)}, u32[]{:S(2)}) async-start(bf16[16,2,256]{2,1,0:T(2,128)(2,1)} %reshape.108), calls=%async_computation.1 | async-start | bytes 32768 | tf_op jit(solution)/shard_map/all_to_all | solution.py:63
  19.3 0.7 %reshape.114 = bf16[2048,1]{0,1:T(2,128)(2,1)S(1)} reshape(bf16[2048]{0:T(1024)(128)(2,1)} %param.15) | data formatting | bytes 8192 | tf_op args[6]
  20.0 0.6 %broadcast.91 = s32[]{:T(128)} broadcast(s32[]{:T(128)} %constant.11.clone.1), dimensions={} | broadcast | bytes 8 | tf_op jit(solution)/shard_map/all_to_all | solution.py:64
  20.6 0.7 %reduce.3 = s32[4,4]{1,0:T(4,128)S(1)} reduce(s32[4,4,1]{1,2,0:T(1,128)S(1)} %all-to-all-done, s32[]{:T(128)} %broadcast.91), dimensions={2}, to_apply=%all_to_all.7.reduce_sub_computation.3 | reduce | bytes 132 | tf_op jit(solution)/shard_map/all_to_all | solution.py:64
  21.3 0.1 eq.48
  21.4 3.5 %all-to-all-done.1 = bf16[16,2,256]{2,1,0:T(2,128)(2,1)S(1)} async-done(((bf16[16,2,256]{2,1,0:T(2,128)(2,1)}), bf16[16,2,256]{2,1,0:T(2,128)(2,1)S(1)}, u32[]{:S(2)}, u32[]{:S(2)}) %all-to-all-start.1) | async-done | bytes 16416 | tf_op jit(solution)/shard_map/all_to_all | solution.py:63
  24.9 0.2 fusion.22
  25.0 0.9 %fusion.20 = (bf16[128,256]{1,0:T(8,128)(2,1)S(1)}, bf16[128,256]{1,0:T(8,128)(2,1)S(1)}) fusion(f32[128,512]{1,0:T(8,128)S(1)} %fusion.22, bf16[1,128,256]{2,1,0:T(8,128)(2,1)} %param.11, bf16[1,128,256]{2,1,0:T(8,128)(2,1)} %param.10), kind=kLoop, calls=%fused_computation.24 | loop fusion | flops 196608 | bytes 524288 | tf_op jit(solution)/shard_map/convert_element_type | solution.py:73
  25.9 5.8 %all_gather.6 = bf16[512,256]{1,0:T(8,128)(2,1)S(1)} all-gather(bf16[128,256]{1,0:T(8,128)(2,1)S(1)} %get-tuple-element.45), channel_id=1, replica_groups=mesh['dp'=4,'ctx'=4,'tp'=2] {'ctx'}, dimensions={0}, use_global_device_ids=true | all-gather | bytes 327680 | tf_op jit(solution)/shard_map/all_gather | solution.py:86
  31.7 5.8 %all_gather.7 = bf16[512,256]{1,0:T(8,128)(2,1)S(1)} all-gather(bf16[128,256]{1,0:T(8,128)(2,1)S(1)} %get-tuple-element.44), channel_id=1, replica_groups=mesh['dp'=4,'ctx'=4,'tp'=2] {'ctx'}, dimensions={0}, use_global_device_ids=true | all-gather | bytes 327680 | tf_op jit(solution)/shard_map/all_gather | solution.py:87
  37.6 9.2 %conditional.1 = (f32[128,2,8]{0,2,1:T(8,128)S(1)}, f32[128,2,8,128]{0,3,2,1:T(8,128)S(1)}) conditional(s32[]{:T(128)} %convert_element_type.53, () %tuple.16, (s32[512]{0:T(512)S(1)}, s32[]{:T(128)}, s32[128]{0:T(128)S(1)}, bf16[512,256]{1,0:T(8,128)(2,1)S(1)}, bf16[1,128,2048]{2,1,0:T(8,128)(2,1)}, /*index=5*/bf16[512,256]{1,0:T(8,128)(2,1)S(1)}) %tuple.17), branch_computations={%region_4.5_spmd, %region_5.8_spmd} | conditional | flops 550836352 | bytes 36007472 | solution.py:101
  37.6 0.1 broadcast_compare_fusion
  37.7 1.1 %copy.44 = bf16[16,8,16,128]{3,2,1,0:T(8,128)(2,1)S(1)} copy(bf16[16,8,16,128]{3,1,2,0:T(8,128)(2,1)} %bitcast.52) | data formatting | bytes 1048576 | tf_op jit(solution)/shard_map/cond
  38.9 0.1 reshape.104
  38.9 0.8 %fusion = (f32[128,2,8]{0,2,1:T(8,128)S(1)}, f32[2,512,128,8]{2,1,3,0:T(8,128)S(1)}) fusion(pred[128,512]{0,1:T(8,128)(4,1)S(1)} %broadcast_compare_fusion, bf16[128,2,8,128]{3,2,1,0:T(8,128)(2,1)S(1)} %bitcast.50, bf16[512,2,128,1]{2,1,0,3:T(2,128)(2,1)S(1)} %bitcast.51), kind=kOutput, calls=%fused_computation.2 | convolution fusion | flops 271579136 | bytes 5054464 | tf_op jit(solution)/shard_map/cond/branch_1_fun/tgrd,sgd->tgrs/dot_general | solution.py:15
  39.7 0.0 copy-start
  39.7 1.9 %copy-done = f32[2,512,128,8]{2,1,3,0:T(8,128)} copy-done((f32[2,512,128,8]{2,1,3,0:T(8,128)}, f32[2,512,128,8]{2,1,3,0:T(8,128)S(1)}, u32[]{:S(2)}) %copy-start) | copy-done | bytes 4194328 | tf_op jit(solution)/shard_map/cond
  41.7 1.0 %fusion.2 = f32[128,2,8]{0,2,1:T(8,128)S(1)} fusion(f32[2,512,128,8]{2,1,3,0:T(8,128)S(1)} %get-tuple-element.43, f32[128,2,8]{0,2,1:T(8,128)S(1)} %broadcast_maximum_fusion, pred[128,512]{0,1:T(8,128)(4,1)S(1)} %broadcast_compare_fusion), kind=kLoop, calls=%fused_computation.4 | loop fusion | flops 5240832 | bytes 4276224 | tf_op jit(solution)/shard_map/cond/branch_1_fun/reduce_sum | solution.py:23
  42.7 0.1 reshape.105
  42.8 3.7 %fusion.9 = f32[128,2,8,128]{3,0,2,1:T(8,128)S(1)} fusion(f32[2,512,128,8]{2,1,3,0:T(8,128)} %copy-done, f32[128,2,8]{0,2,1:T(8,128)S(1)} %broadcast_maximum_fusion, pred[128,512]{0,1:T(8,128)(4,1)S(1)} %broadcast_compare_fusion, f32[128,2,8]{0,2,1:T(8,128)S(1)} %get-tuple-element.40, bf16[512,2,128,1]{2,1,0,3:T(2,128)(2,1)S(1)} %bitcast.53), kind=kOutput, calls=%fused_computation.8 | convolution fusion | flops 273940480 | bytes 5586944 | tf_op jit(solution)/shard_map/cond/branch_1_fun/tgrs,sgd->tgrd/dot_general | solution.py:24
  46.5 0.3 copy.43
  46.8 0.1 divide_convert_fusion
  46.9 1.0 %copy.34 = bf16[1,128,2048]{2,1,0:T(8,128)(2,1)} copy(bf16[1,128,2048]{1,2,0:T(8,128)(2,1)S(1)} %bitcast.48) | data formatting | bytes 1048576
  47.9 0.2 fusion.26
  48.1 5.4 %psum.7 = f32[1,128]{1,0:T(1,128)} all-reduce(f32[1,128]{1,0:T(1,128)S(1)} %fusion.26), channel_id=1, replica_groups=mesh['dp'=4,'ctx'=4,'tp'=2] {'tp'}, use_global_device_ids=true, to_apply=%region_8.9 | all-reduce | flops 128 | bytes 1024 | tf_op jit(solution)/shard_map/psum | solution.py:111
  (7 shorter events, 0.0 us)
Async XLA Ops:
  4.2 11.8 %all-to-all-start = ((s32[4,4,1]{1,2,0:T(1,128)}), s32[4,4,1]{1,2,0:T(1,128)S(1)}, u32[]{:S(2)}, u32[]{:S(2)}) async-start(s32[4,4,1]{1,2,0:T(1,128)} %bitcast.7), calls=%async_computation | async-start | bytes 4096 | tf_op jit(solution)/shard_map/all_to_all | solution.py:64
  16.0 8.8 %all-to-all-start.1 = ((bf16[16,2,256]{2,1,0:T(2,128)(2,1)}), bf16[16,2,256]{2,1,0:T(2,128)(2,1)S(1)}, u32[]{:S(2)}, u32[]{:S(2)}) async-start(bf16[16,2,256]{2,1,0:T(2,128)(2,1)} %reshape.108), calls=%async_computation.1 | async-start | bytes 32768 | tf_op jit(solution)/shard_map/all_to_all | solution.py:63
  39.7 1.9 %copy-start = (f32[2,512,128,8]{2,1,3,0:T(8,128)}, f32[2,512,128,8]{2,1,3,0:T(8,128)S(1)}, u32[]{:S(2)}) copy-start(f32[2,512,128,8]{2,1,3,0:T(8,128)S(1)} %get-tuple-element.43) | copy-start | bytes 12582916 | tf_op jit(solution)/shard_map/cond
where the time goes:
time: 54.1 us; the launch traced here: 53.5 us
  blocking collectives  17 us (31%)
  starting transfers between devices  9.6 us (18%)
  local copies, waits for them, and re-layouts  7.91 us (15%)
  waiting for transfers between devices  7.34 us (14%)
  other arithmetic  5.85 us (11%)
  matrix products  5.05 us (9%)
  between operations  0.68 us (1%)
    all_to_all x1, starting transfers between devices, body(): lax.all_to_all(slot_place, 'dp', split_axis=0, concat_axis=0, tiled=True)  6.35 us
    all_gather x1, blocking collectives, body(): piece_values = lax.all_gather(merged_values, 'ctx', axis=0, tiled=True)  5.84 us
    all_gather x1, blocking collectives, body(): piece_keys = lax.all_gather(merged_keys, 'ctx', axis=0, tiled=True)  5.78 us
    psum x1, blocking collectives, body(): value_out = lax.psum(partial_value, 'tp')  5.42 us
    all_to_all x1, waiting for transfers between devices, body(): lax.all_to_all(slot_place, 'dp', split_axis=0, concat_axis=0, tiled=True)  3.85 us
    dot_general x1, matrix products, attend_block(): jnp.einsum('tgrs,sgd->tgrd', weights.astype(jnp.bfloat16), block_values,...  3.67 us
    all_to_all x1, waiting for transfers between devices, body(): lax.all_to_all(packed, 'dp', split_axis=0, concat_axis=0, tiled=True)  3.49 us
    all_to_all x1, starting transfers between devices, body(): lax.all_to_all(packed, 'dp', split_axis=0, concat_axis=0, tiled=True)  3.25 us
  transfers between devices with their start and end apart: 2, of which 2 were waited for; matrix products, arithmetic and copies ran while one was open for 7% of the time, Pallas kernels for 0%

commit v1 on v0

--- a/solution.py
+++ b/solution.py
@@ -83,7 +83,12 @@
     )
     carried = initial
     start_row = jnp.int32(0)
-    piece_keys = lax.all_gather(merged_keys, "ctx", axis=0, tiled=True)
+    ring = [merged_keys]
+    for hop in range(3):
+        ring.append(lax.ppermute(ring[-1], "ctx", [(dev, (dev + 1) % 4) for dev in range(4)]))
+    piece_keys = jnp.roll(
+        jnp.concatenate(ring[::-1], axis=0), (lax.axis_index("ctx") + 1) * ring[0].shape[0], axis=0
+    )
     piece_values = lax.all_gather(merged_values, "ctx", axis=0, tiled=True)
     piece_rows = piece_keys.shape[0]
     block_rows = min(512, piece_rows)

time: 54.1 us -> 56.6 us (1.046)
  waiting for transfers between devices: 7.34 us -> 14.8 us
  blocking collectives: 17 us -> 11.6 us
    ppermute x0 -> x3, waiting for transfers between devices: none -> 6.67 us  [body(): lax.ppermute(ring[-1], 'ctx', [(dev, (dev + 1) % 4) for dev in range(4)])]
    all_gather x1 -> x0, blocking collectives: 5.78 us -> none  [body(): piece_keys = lax.all_gather(merged_keys, 'ctx', axis=0, tiled=True)]
    all_to_all x1, waiting for transfers between devices: 3.49 us -> 4.32 us  [body(): lax.all_to_all(packed, 'dp', split_axis=0, concat_axis=0, tiled=True)]
    unnamed x4 -> x11, local copies, waits for them, and re-layouts: 2.41 us -> 2.46 us
  transfers between devices with their start and end apart: 2 -> 5, of which waited for: 2 -> 4; matrix products, arithmetic and copies ran while one was open for 7% -> 6% of each run, Pallas kernels for 0% -> 0%
where the time goes in v1:
time: 56.6 us; the launch traced here: 56.1 us
  waiting for transfers between devices  14.8 us (26%)
  blocking collectives  11.6 us (20%)
  starting transfers between devices  9.66 us (17%)
  local copies, waits for them, and re-layouts  8.18 us (14%)
  other arithmetic  5.81 us (10%)
  matrix products  5.14 us (9%)
  between operations  0.76 us (1%)
    ppermute x3, waiting for transfers between devices, body(): lax.ppermute(ring[-1], 'ctx', [(dev, (dev + 1) % 4) for dev in range(4)])  6.67 us
    all_to_all x1, starting transfers between devices, body(): lax.all_to_all(slot_place, 'dp', split_axis=0, concat_axis=0, tiled=True)  6.35 us
    all_gather x1, blocking collectives, body(): piece_values = lax.all_gather(merged_values, 'ctx', axis=0, tiled=True)  6.21 us
    psum x1, blocking collectives, body(): value_out = lax.psum(partial_value, 'tp')  5.42 us
    all_to_all x1, waiting for transfers between devices, body(): lax.all_to_all(packed, 'dp', split_axis=0, concat_axis=0, tiled=True)  4.32 us
    all_to_all x1, waiting for transfers between devices, body(): lax.all_to_all(slot_place, 'dp', split_axis=0, concat_axis=0, tiled=True)  3.85 us
    dot_general x1, matrix products, attend_block(): jnp.einsum('tgrs,sgd->tgrd', weights.astype(jnp.bfloat16), block_values,...  3.67 us
    all_to_all x1, starting transfers between devices, body(): lax.all_to_all(packed, 'dp', split_axis=0, concat_axis=0, tiled=True)  3.25 us
  transfers between devices with their start and end apart: 5, of which 4 were waited for; matrix products, arithmetic and copies ran while one was open for 6% of the time, Pallas kernels for 0%

profile of v1, /device:TPU:0, one launch (start us, length us, event | category | flops | bytes accessed | tf_op | source)
XLA Modules:
  0.0 56.1 jit_solution(10868257774627822605)
XLA Ops:
  0.6 0.7 %fusion.24 = s32[8,4]{0,1:T(4,128)S(1)} fusion(s32[8]{0:T(128)} %bitcast.63), kind=kLoop, calls=%fused_computation.45 | loop fusion | flops 64 | bytes 160 | tf_op jit(solution)/shard_map/convert_element_type | solution.py:48
  1.3 0.2 reduce_window_sum.11
  1.5 0.7 %select_reduce_fusion.1 = s32[8]{0:T(128)S(1)} fusion(s32[8,4]{0,1:T(4,128)S(1)} %reduce_window_sum.11, s32[8]{0:T(128)} %bitcast.64), kind=kLoop, calls=%fused_computation.43 | loop fusion | flops 152 | bytes 192 | tf_op jit(solution)/shard_map/reduce_sum | solution.py:52
  2.2 0.7 %multiply_add_fusion.1 = s32[8]{0:T(128)S(1)} fusion(s32[8]{0:T(128)S(1)} %select_reduce_fusion.1, s32[1,1,8,1]{2,3,1,0:T(1,128)} %param.13), kind=kLoop, calls=%fused_computation.47 | loop fusion | flops 16 | bytes 96 | tf_op jit(solution)/shard_map/add | solution.py:53
  2.8 0.7 %convert_reduce_fusion = (s32[16]{0:T(128)S(1)}, s32[16]{0:T(128)S(1)}) fusion(s32[8]{0:T(128)S(1)} %multiply_add_fusion.1, s32[8]{0:T(128)} %bitcast.65), kind=kLoop, calls=%fused_computation.39 | loop fusion | flops 608 | bytes 192 | tf_op jit(solution)/shard_map/reduce_sum | solution.py:59
  3.6 0.7 %add.77 = s32[4,4,1]{1,0,2:T(4,128)} reshape(s32[16]{0:T(128)S(1)} %multiply_add_fusion) | data formatting | bytes 128 | tf_op jit(solution)/shard_map/add | solution.py:60
  4.2 6.3 %all-to-all-start = ((s32[4,4,1]{1,2,0:T(1,128)}), s32[4,4,1]{1,2,0:T(1,128)S(1)}, u32[]{:S(2)}, u32[]{:S(2)}) async-start(s32[4,4,1]{1,2,0:T(1,128)} %bitcast.3), calls=%async_computation | async-start | bytes 4096 | tf_op jit(solution)/shard_map/all_to_all | solution.py:64
  10.6 0.7 %copy.48 = bf16[1,8,2,256]{3,1,2,0:T(8,128)(2,1)S(1)} copy(bf16[1,8,2,256]{3,2,1,0:T(2,128)(2,1)} %bitcast.61) | data formatting | bytes 16384
  11.3 0.3 convolution_convert_fusion
  11.5 0.6 %reshape.115 = bf16[16,2,256]{2,1,0:T(2,128)(2,1)} reshape(bf16[16,512]{1,0:T(8,128)(2,1)S(1)} %convolution_convert_fusion) | data formatting | bytes 32768 | tf_op jit(solution)/shard_map/reshape | solution.py:61
  12.2 3.8 %all-to-all-done = s32[4,4,1]{1,2,0:T(1,128)S(1)} async-done(((s32[4,4,1]{1,2,0:T(1,128)}), s32[4,4,1]{1,2,0:T(1,128)S(1)}, u32[]{:S(2)}, u32[]{:S(2)}) %all-to-all-start) | async-done | bytes 96 | tf_op jit(solution)/shard_map/all_to_all | solution.py:64
  16.0 3.3 %all-to-all-start.1 = ((bf16[16,2,256]{2,1,0:T(2,128)(2,1)}), bf16[16,2,256]{2,1,0:T(2,128)(2,1)S(1)}, u32[]{:S(2)}, u32[]{:S(2)}) async-start(bf16[16,2,256]{2,1,0:T(2,128)(2,1)} %reshape.115), calls=%async_computation.1 | async-start | bytes 32768 | tf_op jit(solution)/shard_map/all_to_all | solution.py:63
  19.3 0.5 broadcast.106
  19.8 0.7 %reduce.3 = s32[4,4]{1,0:T(4,128)S(1)} reduce(s32[4,4,1]{1,2,0:T(1,128)S(1)} %all-to-all-done, s32[]{:T(128)} %broadcast.106), dimensions={2}, to_apply=%all_to_all.7.reduce_sub_computation.3 | reduce | bytes 132 | tf_op jit(solution)/shard_map/all_to_all | solution.py:64
  20.4 0.1 eq.51
  20.5 4.3 %all-to-all-done.1 = bf16[16,2,256]{2,1,0:T(2,128)(2,1)S(1)} async-done(((bf16[16,2,256]{2,1,0:T(2,128)(2,1)}), bf16[16,2,256]{2,1,0:T(2,128)(2,1)S(1)}, u32[]{:S(2)}, u32[]{:S(2)}) %all-to-all-start.1) | async-done | bytes 16416 | tf_op jit(solution)/shard_map/all_to_all | solution.py:63
  24.9 0.2 fusion.21
  25.0 0.9 %fusion.19 = (bf16[128,256]{1,0:T(8,128)(2,1)S(1)}, bf16[128,256]{1,0:T(8,128)(2,1)S(1)}) fusion(f32[128,512]{1,0:T(8,128)S(1)} %fusion.21, bf16[1,128,256]{2,1,0:T(8,128)(2,1)} %param.11, bf16[1,128,256]{2,1,0:T(8,128)(2,1)} %param.10), kind=kLoop, calls=%fused_computation.24 | loop fusion | flops 196608 | bytes 524288 | tf_op jit(solution)/shard_map/convert_element_type | solution.py:73
  25.9 0.1 collective-permute-start
  26.0 3.7 %collective-permute-done = bf16[128,256]{1,0:T(8,128)(2,1)S(1)} collective-permute-done((bf16[128,256]{1,0:T(8,128)(2,1)S(1)}, bf16[128,256]{1,0:T(8,128)(2,1)S(1)}, u32[]{:S(2)}, u32[]{:S(2)}) %collective-permute-start) | collective-permute-done | bytes 65568 | tf_op jit(solution)/shard_map/ppermute | solution.py:88
  29.7 0.0 collective-permute-start.1
  29.7 0.7 %reshape.123 = bf16[2048,1]{0,1:T(2,128)(2,1)S(1)} reshape(bf16[2048]{0:T(1024)(128)(2,1)} %param.15) | data formatting | bytes 8192 | tf_op args[6]
  30.4 3.0 %collective-permute-done.1 = bf16[128,256]{1,0:T(8,128)(2,1)S(1)} collective-permute-done((bf16[128,256]{1,0:T(8,128)(2,1)S(1)}, bf16[128,256]{1,0:T(8,128)(2,1)S(1)}, u32[]{:S(2)}, u32[]{:S(2)}) %collective-permute-start.1) | collective-permute-done | bytes 65568 | tf_op jit(solution)/shard_map/ppermute | solution.py:88
  33.4 0.0 collective-permute-start.2
  33.4 6.2 %all_gather.3 = bf16[512,256]{1,0:T(8,128)(2,1)S(1)} all-gather(bf16[128,256]{1,0:T(8,128)(2,1)S(1)} %get-tuple-element.201), channel_id=1, replica_groups=mesh['dp'=4,'ctx'=4,'tp'=2] {'ctx'}, dimensions={0}, use_global_device_ids=true | all-gather | bytes 327680 | tf_op jit(solution)/shard_map/all_gather | solution.py:92
  39.6 0.0 collective-permute-done.2
  39.7 9.7 %conditional.1 = (f32[128,2,8]{0,2,1:T(8,128)S(1)}, f32[128,2,8,128]{0,3,2,1:T(8,128)S(1)}) conditional(s32[]{:T(128)} %convert_element_type.56, () %tuple.27, (s32[512]{0:T(512)S(1)}, s32[]{:T(128)}, s32[128]{0:T(128)S(1)}, s32[]{:T(128)}, s32[]{:T(128)}, /*index=5*/bf16[1024,256]{1,0:T(8,128)(2,1)S(1)}, bf16[1,128,2048]{2,1,0:T(8,128)(2,1)}, ...), branch_computations={%region_4.5_spmd, %region_5.8_spmd.clone} | conditional | flops 550836352 | bytes 37056208 | solution.py:106
  39.7 0.1 broadcast_compare_fusion
  39.9 0.2 copy.35
  40.1 0.2 constant_dynamic-slice_fusion
  40.3 1.1 %copy.47 = bf16[16,8,16,128]{3,2,1,0:T(8,128)(2,1)S(1)} copy(bf16[16,8,16,128]{3,1,2,0:T(8,128)(2,1)} %bitcast.57) | data formatting | bytes 1048576 | tf_op jit(solution)/shard_map/cond
  41.4 0.9 %fusion = (f32[128,2,8]{0,2,1:T(8,128)S(1)}, f32[2,512,128,8]{2,1,3,0:T(8,128)S(1)}) fusion(pred[128,512]{0,1:T(8,128)(4,1)S(1)} %broadcast_compare_fusion, bf16[512,2,128,1]{0,2,3,1:T(8,128)(2,1)S(1)} %bitcast.56, bf16[128,2,8,128]{3,2,1,0:T(8,128)(2,1)S(1)} %bitcast.55), kind=kOutput, calls=%fused_computation.2 | convolution fusion | flops 271579136 | bytes 5054464 | tf_op jit(solution)/shard_map/cond/branch_1_fun/tgrd,sgd->tgrs/dot_general | solution.py:15
  42.3 0.0 copy-start
  42.3 1.9 %copy-done = f32[2,512,128,8]{2,1,3,0:T(8,128)} copy-done((f32[2,512,128,8]{2,1,3,0:T(8,128)}, f32[2,512,128,8]{2,1,3,0:T(8,128)S(1)}, u32[]{:S(2)}) %copy-start) | copy-done | bytes 4194328 | tf_op jit(solution)/shard_map/cond
  44.2 1.0 %fusion.2 = f32[128,2,8]{0,2,1:T(8,128)S(1)} fusion(f32[2,512,128,8]{2,1,3,0:T(8,128)S(1)} %get-tuple-element.200, f32[128,2,8]{0,2,1:T(8,128)S(1)} %broadcast_maximum_fusion, pred[128,512]{0,1:T(8,128)(4,1)S(1)} %broadcast_compare_fusion), kind=kLoop, calls=%fused_computation.4 | loop fusion | flops 5240832 | bytes 4276224 | tf_op jit(solution)/shard_map/cond/branch_1_fun/reduce_sum | solution.py:23
  45.3 0.1 reshape.118
  45.4 3.7 %fusion.9 = f32[128,2,8,128]{3,0,2,1:T(8,128)S(1)} fusion(f32[2,512,128,8]{2,1,3,0:T(8,128)} %copy-done, f32[128,2,8]{0,2,1:T(8,128)S(1)} %broadcast_maximum_fusion, pred[128,512]{0,1:T(8,128)(4,1)S(1)} %broadcast_compare_fusion, f32[128,2,8]{0,2,1:T(8,128)S(1)} %get-tuple-element.197, bf16[512,2,128,1]{2,1,0,3:T(2,128)(2,1)S(1)} %bitcast.58), kind=kOutput, calls=%fused_computation.8 | convolution fusion | flops 273940480 | bytes 5586944 | tf_op jit(solution)/shard_map/cond/branch_1_fun/tgrs,sgd->tgrd/dot_general | solution.py:24
  49.0 0.3 copy.46
  49.4 0.1 divide_convert_fusion
  49.5 1.0 %copy.37 = bf16[1,128,2048]{2,1,0:T(8,128)(2,1)} copy(bf16[1,128,2048]{1,2,0:T(8,128)(2,1)S(1)} %bitcast.53) | data formatting | bytes 1048576
  50.5 0.2 fusion.25
  50.7 5.4 %psum.7 = f32[1,128]{1,0:T(1,128)} all-reduce(f32[1,128]{1,0:T(1,128)S(1)} %fusion.25), channel_id=1, replica_groups=mesh['dp'=4,'ctx'=4,'tp'=2] {'tp'}, use_global_device_ids=true, to_apply=%region_8.9 | all-reduce | flops 128 | bytes 1024 | tf_op jit(solution)/shard_map/psum | solution.py:116
  (15 shorter events, 0.1 us)
Async XLA Ops:
  4.2 11.8 %all-to-all-start = ((s32[4,4,1]{1,2,0:T(1,128)}), s32[4,4,1]{1,2,0:T(1,128)S(1)}, u32[]{:S(2)}, u32[]{:S(2)}) async-start(s32[4,4,1]{1,2,0:T(1,128)} %bitcast.3), calls=%async_computation | async-start | bytes 4096 | tf_op jit(solution)/shard_map/all_to_all | solution.py:64
  16.0 8.8 %all-to-all-start.1 = ((bf16[16,2,256]{2,1,0:T(2,128)(2,1)}), bf16[16,2,256]{2,1,0:T(2,128)(2,1)S(1)}, u32[]{:S(2)}, u32[]{:S(2)}) async-start(bf16[16,2,256]{2,1,0:T(2,128)(2,1)} %reshape.115), calls=%async_computation.1 | async-start | bytes 32768 | tf_op jit(solution)/shard_map/all_to_all | solution.py:63
  25.9 3.7 %collective-permute-start = (bf16[128,256]{1,0:T(8,128)(2,1)S(1)}, bf16[128,256]{1,0:T(8,128)(2,1)S(1)}, u32[]{:S(2)}, u32[]{:S(2)}) collective-permute-start(bf16[128,256]{1,0:T(8,128)(2,1)S(1)} %get-tuple-element.202), channel_id=1, source_target_pairs={{0,2},{2,4},{4,6},{6,0},{1,3},{3,5},{5,7},{7,1},{8,10},{10,12},{12... | collective-permute-start | bytes 196616 | tf_op jit(solution)/shard_map/ppermute | solution.py:88
  29.7 3.7 %collective-permute-start.1 = (bf16[128,256]{1,0:T(8,128)(2,1)S(1)}, bf16[128,256]{1,0:T(8,128)(2,1)S(1)}, u32[]{:S(2)}, u32[]{:S(2)}) collective-permute-start(bf16[128,256]{1,0:T(8,128)(2,1)S(1)} %collective-permute-done), channel_id=1, source_target_pairs={{0,2},{2,4},{4,6},{6,0},{1,3},{3,5},{5,7},{7,1},{8,10},{10,12},{12... | collective-permute-start | bytes 196616 | tf_op jit(solution)/shard_map/ppermute | solution.py:88
  33.4 6.2 %collective-permute-start.2 = (bf16[128,256]{1,0:T(8,128)(2,1)S(1)}, bf16[128,256]{1,0:T(8,128)(2,1)S(1)}, u32[]{:S(2)}, u32[]{:S(2)}) collective-permute-start(bf16[128,256]{1,0:T(8,128)(2,1)S(1)} %collective-permute-done.1), channel_id=1, source_target_pairs={{0,2},{2,4},{4,6},{6,0},{1,3},{3,5},{5,7},{7,1},{8,10},{10,12},{12... | collective-permute-start | bytes 196616 | tf_op jit(solution)/shard_map/ppermute | solution.py:88
  42.3 1.9 %copy-start = (f32[2,512,128,8]{2,1,3,0:T(8,128)}, f32[2,512,128,8]{2,1,3,0:T(8,128)S(1)}, u32[]{:S(2)}) copy-start(f32[2,512,128,8]{2,1,3,0:T(8,128)S(1)} %get-tuple-element.200) | copy-start | bytes 12582916 | tf_op jit(solution)/shard_map/cond
